TPU v7x, 32 devices: a whole 2x2x4 slice. The times are simulated.
32 devices in a mesh: scen: 8 (over z, x), rootr: 2 (over core), rootc: 2 (over y).
Axes of the slice: x: 2, y: 2, z: 4, core: 2. Of those that a mesh axis runs over, the one named last changes fastest.
Arguments:
- start_guess: float32 [8192, 256], P(('scen', 'rootr'), 'rootc'), may hold values from -6 to 6
- right_side: float32 [8192, 256], P(('scen', 'rootr'), 'rootc'), may hold values from -6 to 6
- root_diagonal: float32 [8192], P(('scen', 'rootr')), may hold values from 1 to 4
- preconditioner: bfloat16 [8192, 8192], P(('scen', 'rootr')), may hold values from -0.015625 to 0.015625
- border_block: bfloat16 [16, 512, 768], P(('scen', 'rootr'), 'rootc'), may hold values from -0.21875 to 0.21875
- coupling_inverse: bfloat16 [16, 512, 512], P(('scen', 'rootr'), 'rootc'), may hold values from -0.25 to 0.25
- border_count: int32 [16], P(('scen', 'rootr')), may hold values from 64 to 512, as said below
- column_tiles: int32 [16, 6], P(('scen', 'rootr')), may hold values from 0 to 63, as said below
Outputs:
- final_iterate: float32 [8192, 256], P(('scen', 'rootr'), 'rootc')
Inputs may be any that keep to these rules, and one draw needn't show every extreme that they name: A scenario's live border rows are its first border_count rows; some scenario has exactly 512. `column_tiles`: each row names 6 different tiles in rising order.
All inputs are finite; a program needn't handle non-finite values.
Results may differ from a plain program's by a relative error of at most 0.0022.
Values may be sent and summed in bfloat16 or wider, within the bound.
A program may use at most 64 MiB of HBM per device.

v0:
```python
import jax
import jax.numpy as jnp
from jax import lax
from jax.sharding import PartitionSpec as P

TILE = 128


def border_product(matrix, operand, live_here):
    half_rows = matrix.shape[0]
    live_mask = (jnp.arange(half_rows) < live_here)[:, None]
    product = jnp.dot(matrix, operand, preferred_element_type=jnp.float32)
    return jnp.where(live_mask, product, 0.0).astype(jnp.bfloat16)


def border_transpose(border, solved):
    numbers = (((0,), (0,)), ((), ()))
    return lax.dot_general(border, solved, numbers, preferred_element_type=jnp.float32)


def local(
    start_guess,
    right_side,
    root_diagonal,
    preconditioner,
    border_block,
    coupling_inverse,
    border_count,
    column_tiles,
):
    own_rows = start_guess.shape[0]
    half_rhs = start_guess.shape[1]
    half_rows = border_block.shape[1]
    coupled_cols = border_block.shape[2]
    order_rows = preconditioner.shape[1]
    border = border_block[0]
    inverse_rows = coupling_inverse[0]
    tile_ids = column_tiles[0]
    offset = lax.axis_index("rootc") * half_rows
    live_here = jnp.clip(border_count[0] - offset, 0, half_rows)
    iterate = start_guess
    own_low = iterate.astype(jnp.bfloat16)
    both_halves = lax.all_gather(own_low, "rootc", axis=1, tiled=True)
    gathered = lax.all_gather(both_halves, ("scen", "rootr"), axis=0, tiled=True)
    all_rhs = gathered.shape[1]
    picked = gathered.reshape(order_rows // TILE, TILE, all_rhs)[tile_ids].reshape(
        coupled_cols, all_rhs
    )
    values_local = border_product(border, picked, live_here)
    values_whole = lax.all_gather(values_local, "rootc", axis=0, tiled=True)
    solved = border_product(inverse_rows, values_whole, live_here)
    term_part = border_transpose(border, solved)
    term_half = lax.psum_scatter(term_part, "rootc", scatter_dimension=1, tiled=True)
    spread_terms = jnp.zeros((order_rows // TILE, TILE, half_rhs), jnp.float32)
    spread_terms = (
        spread_terms.at[tile_ids]
        .add(term_half.reshape(-1, TILE, half_rhs))
        .reshape(order_rows, half_rhs)
    )
    own_terms = right_side - root_diagonal[:, None] * iterate
    first_row = lax.axis_index(("scen", "rootr")) * own_rows
    current = lax.dynamic_slice_in_dim(spread_terms, first_row, own_rows, 0)
    spread_terms = lax.dynamic_update_slice_in_dim(spread_terms, current + own_terms, first_row, 0)
    residual = lax.psum(spread_terms, ("scen", "rootr"))
    update = jnp.dot(
        preconditioner, residual.astype(jnp.bfloat16), preferred_element_type=jnp.float32
    )
    iterate = iterate + update
    return iterate


def solution(mesh):
    placed = (
        P(("scen", "rootr"), "rootc"),
        P(("scen", "rootr"), "rootc"),
        P(("scen", "rootr")),
        P(("scen", "rootr"), None),
        P(("scen", "rootr"), "rootc", None),
        P(("scen", "rootr"), "rootc", None),
        P(("scen", "rootr")),
        P(("scen", "rootr"), None),
    )
    return jax.shard_map(
        local, mesh=mesh, in_specs=placed, out_specs=P(("scen", "rootr"), "rootc"), check_vma=False
    )
```

profile of v0, /device:TPU:1, one launch (start us, length us, event | category | flops | bytes accessed | tf_op | source)
XLA Modules:
  0.0 212.2 jit_solution(9271630107999515381)
XLA Ops:
  6.5 0.0 copy-start
  6.5 0.0 copy-start.1
  6.5 0.0 all-gather.2.cloned.1.call-start
  6.5 1.0 convert_element_type.16
  7.6 6.1 %all_gather.9 = bf16[512,256]{1,0:T(8,128)(2,1)} all-gather(bf16[512,128]{1,0:T(8,128)(2,1)S(1)} %convert_element_type.16), channel_id=1, replica_groups=mesh['scen'=8,'rootr'=2,'rootc'=2] {'rootc'}, dimensions={1}, use_global_device_ids=true | all-gather | bytes 393216 | tf_op jit(solution)/shard_map/all_gather | solution.py:43
  13.6 0.0 all-gather.2.cloned.1.call-update
  13.7 0.0 reduce-scatter.2.cloned.1.call-start
  14.4 0.7 fusion.17
  15.0 51.6 %all-gather.2.cloned.1.call-done = bf16[8192,256]{1,0:T(8,128)(2,1)} async-done(((bf16[512,256]{1,0:T(8,128)(2,1)}), bf16[8192,256]{1,0:T(8,128)(2,1)}) %all-gather.2.cloned.1.call-update) | async-done | bytes 4194320 | tf_op jit(solution)/shard_map/all_gather | solution.py:44
  66.7 2.8 %gather_fusion = bf16[6,128,256]{2,1,0:T(8,128)(2,1)S(1)} fusion(bf16[64,128,256]{2,1,0:T(8,128)(2,1)} %bitcast.34, s32[1024]{0:T(1024)S(1)} %pad_clamp_fusion), kind=kCustom, calls=%fused_computation | custom fusion | bytes 786456 | tf_op jit(solution)/shard_map/gather | solution.py:46
  69.4 0.0 copy-done
  69.4 0.3 fusion.10
  69.8 5.4 %all_gather.11 = bf16[512,256]{0,1:T(8,128)(2,1)S(1)} all-gather(bf16[256,256]{0,1:T(8,128)(2,1)S(1)} %fusion.10), channel_id=1, replica_groups=mesh['scen'=8,'rootr'=2,'rootc'=2] {'rootc'}, dimensions={0}, use_global_device_ids=true | all-gather | bytes 393216 | tf_op jit(solution)/shard_map/all_gather | solution.py:50
  75.2 0.0 copy-start.2
  75.2 0.0 copy-start.3
  75.2 2.4 %convolution_bitcast_fusion = f32[768,256]{0,1:T(8,128)} fusion(bf16[512,256]{0,1:T(8,128)(2,1)S(1)} %all_gather.11, bf16[1,256,768]{2,1,0:T(8,128)(2,1)S(1)} %copy-done, bf16[1,256,512]{2,1,0:T(8,128)(2,1)} %param.13, pred[256]{0:T(512)(128)(4,1)S(1)} %iota_compare_fusion), kind=kOutput, calls=%fused_computation.4 | convolution fusion | flops 167903232 | bytes 1704192 | tf_op jit(solution)/shard_map/dot_general | solution.py:18
  77.7 0.0 reduce-scatter.2.cloned.1.call-update
  77.7 0.0 copy-done.1
  77.7 0.1 copy.12
  77.8 16.3 %reduce-scatter.2.cloned.1.call-done = f32[768,128]{0,1:T(8,128)} async-done(((f32[768,256]{0,1:T(8,128)}), f32[768,128]{0,1:T(8,128)}) %reduce-scatter.2.cloned.1.call-update) | async-done | bytes 393232 | tf_op jit(solution)/shard_map/reduce_scatter | solution.py:53
  94.2 1.1 copy.11
  95.3 2.5 %broadcast_in_dim.24 = f32[64,128,128]{2,1,0:T(8,128)} broadcast(f32[]{:T(128)} %constant.10.clone.1), dimensions={} | broadcast | bytes 4194308 | tf_op jit(solution)/shard_map/broadcast_in_dim | solution.py:54
  97.8 2.6 %scatter_fusion = f32[64,128,128]{2,1,0:T(8,128)} fusion(f32[64,128,128]{2,1,0:T(8,128)} %broadcast_in_dim.24, s32[6]{0:T(128)S(1)} %fusion.17, f32[6,128,128]{2,1,0:T(8,128)S(1)} %bitcast.32), kind=kCustom, calls=%fused_computation.1 | custom fusion | flops 98304 | bytes 1179672 | tf_op jit(solution)/shard_map/scatter-add | solution.py:57
  100.4 0.0 copy-done.2
  100.4 0.0 copy-done.3
  100.4 1.8 add_dynamic-update-slice_fusion
  102.1 96.1 %all-reduce.1 = bf16[8192,128]{1,0:T(8,128)(2,1)S(1)} all-reduce(f32[8192,128]{1,0:T(8,128)} %add_dynamic-update-slice_fusion), channel_id=1, replica_groups=mesh['scen'=8,'rootr'=2,'rootc'=2] {'scen','rootr'}, use_global_device_ids=true, to_apply=%region_2.3 | all-reduce | flops 1048576 | bytes 6291456 | tf_op jit(solution)/shard_map/psum | solution.py:64
  198.2 6.3 %fusion.5 = f32[512,128]{0,1:T(8,128)S(1)} fusion(f32[512,128]{0,1:T(8,128)S(1)} %copy.12, bf16[512,8192]{1,0:T(8,128)(2,1)} %param.11, bf16[8192,128]{1,0:T(8,128)(2,1)S(1)} %all-reduce.1), kind=kOutput, calls=%fused_computation.8 | convolution fusion | flops 1073807360 | bytes 11010048 | tf_op jit(solution)/shard_map/dot_general | solution.py:65
  204.5 0.8 copy.13
  (2 shorter events, 0.0 us)
Async XLA Ops:
  6.5 62.9 %copy-start = (bf16[1,256,768]{2,1,0:T(8,128)(2,1)S(1)}, bf16[1,256,768]{2,1,0:T(8,128)(2,1)}, u32[]{:S(2)}) copy-start(bf16[1,256,768]{2,1,0:T(8,128)(2,1)} %param.12) | copy-start | bytes 1179652
  6.5 71.1 %copy-start.1 = (f32[512,128]{1,0:T(8,128)S(1)}, f32[512,128]{1,0:T(8,128)}, u32[]{:S(2)}) copy-start(f32[512,128]{1,0:T(8,128)} %param.8) | copy-start | bytes 786436
  6.5 60.1 %all-gather.2.cloned.1.call-start = ((), (), s32[]{:S(2)}) async-start(), calls=%async_computation.1 | async-start | bytes 4456448 | tf_op jit(solution)/shard_map/all_gather | solution.py:44
  13.7 80.5 %reduce-scatter.2.cloned.1.call-start = ((), (), s32[]{:S(2)}) async-start(), calls=%async_computation.2 | async-start | bytes 1179648 | tf_op jit(solution)/shard_map/reduce_scatter | solution.py:53
  75.2 25.2 %copy-start.2 = (f32[512,128]{1,0:T(8,128)S(1)}, f32[512,128]{1,0:T(8,128)}, u32[]{:S(2)}) copy-start(f32[512,128]{1,0:T(8,128)} %param.9) | copy-start | bytes 786436
  75.2 25.2 %copy-start.3 = (f32[512]{0:T(512)S(1)}, f32[512]{0:T(512)}, u32[]{:S(2)}) copy-start(f32[512]{0:T(512)} %param.10) | copy-start | bytes 6148
Sparse Core Ops, SparseCore 0:
  13.8 52.8 all-gather.1
  77.8 16.3 reduce-scatter.1
where the time goes:
time: 213 us; the launch traced here: 212 us
  blocking collectives  108 us (51%)
  waiting for transfers between devices  68 us (32%)
  between operations  14.1 us (7%)
  matrix products  9.04 us (4%)
  local copies, waits for them, and re-layouts  7.34 us (3%)
  other arithmetic  6.06 us (3%)
    psum x1, blocking collectives, local(): residual = lax.psum(spread_terms, ('scen', 'rootr'))  96.1 us
    all_gather x1, waiting for transfers between devices, local(): lax.all_gather(both_halves, ('scen', 'rootr'), axis=0, tiled=True)  51.6 us
    reduce_scatter x1, waiting for transfers between devices, local(): lax.psum_scatter(term_part, 'rootc', scatter_dimension=1, tiled=True)  16.3 us
    dot_general x1, matrix products, local(): jnp.dot(preconditioner, residual.astype(jnp.bfloat16), preferred_element_...  6.28 us
    all_gather x1, blocking collectives, local(): both_halves = lax.all_gather(own_low, 'rootc', axis=1, tiled=True)  6.05 us
    all_gather x1, blocking collectives, local(): values_whole = lax.all_gather(values_local, 'rootc', axis=0, tiled=True)  5.45 us
  transfers between devices with their start and end apart: 2, of which 2 were waited for; matrix products, arithmetic and copies ran while one was open for 0% of the time, Pallas kernels for 0%

commit v1 on v0

--- a/solution.py
+++ b/solution.py
@@ -2,6 +2,7 @@
 import jax.numpy as jnp
 from jax import lax
 from jax.sharding import PartitionSpec as P
+from jax.lax import psum
 
 TILE = 128
 
@@ -61,7 +62,8 @@
     first_row = lax.axis_index(("scen", "rootr")) * own_rows
     current = lax.dynamic_slice_in_dim(spread_terms, first_row, own_rows, 0)
     spread_terms = lax.dynamic_update_slice_in_dim(spread_terms, current + own_terms, first_row, 0)
-    residual = lax.psum(spread_terms, ("scen", "rootr"))
+    tracks_press = lambda a0, link_axis, axis_id: psum(psum(a0, link_axis), axis_name=axis_id)
+    residual = tracks_press(spread_terms, "rootr", "scen")
     update = jnp.dot(
         preconditioner, residual.astype(jnp.bfloat16), preferred_element_type=jnp.float32
     )

time: 213 us -> 313 us (1.47)
  blocking collectives: 108 us -> 179 us
  waiting for transfers between devices: 68 us -> 96.8 us
    psum x1, blocking collectives: 96.1 us -> 167 us  [local(): psum(psum(a0, link_axis), axis_name=axis_id)]
    psum x0 -> x1, waiting for transfers between devices: none -> 28.7 us  [local(): psum(a0, link_axis)]
  transfers between devices with their start and end apart: 2 -> 3, of which waited for: 2 -> 3; matrix products, arithmetic and copies ran while one was open for 0% -> 0% of each run, Pallas kernels for 0% -> 0%
where the time goes in v1:
time: 313 us; the launch traced here: 312 us
  blocking collectives  179 us (57%)
  waiting for transfers between devices  96.8 us (31%)
  between operations  13.8 us (4%)
  matrix products  9.05 us (3%)
  local copies, waits for them, and re-layouts  7.37 us (2%)
  other arithmetic  6.06 us (2%)
    psum x1, blocking collectives, local(): psum(psum(a0, link_axis), axis_name=axis_id)  167 us
    all_gather x1, waiting for transfers between devices, local(): lax.all_gather(both_halves, ('scen', 'rootr'), axis=0, tiled=True)  51.6 us
    psum x1, waiting for transfers between devices, local(): psum(a0, link_axis)  28.7 us
    reduce_scatter x1, waiting for transfers between devices, local(): lax.psum_scatter(term_part, 'rootc', scatter_dimension=1, tiled=True)  16.4 us
    dot_general x1, matrix products, local(): jnp.dot(preconditioner, residual.astype(jnp.bfloat16), preferred_element_...  6.28 us
  transfers between devices with their start and end apart: 3, of which 3 were waited for; matrix products, arithmetic and copies ran while one was open for 0% of the time, Pallas kernels for 0%

profile of v1, /device:TPU:1, one launch (start us, length us, event | category | flops | bytes accessed | tf_op | source)
XLA Modules:
  0.0 311.7 jit_solution(3829483338112859500)
XLA Ops:
  6.5 0.0 copy-start
  6.5 0.0 all-gather.2.cloned.1.call-start
  6.5 1.0 convert_element_type.16
  7.6 6.1 %all_gather.9 = bf16[512,256]{1,0:T(8,128)(2,1)} all-gather(bf16[512,128]{1,0:T(8,128)(2,1)S(1)} %convert_element_type.16), channel_id=1, replica_groups=mesh['scen'=8,'rootr'=2,'rootc'=2] {'rootc'}, dimensions={1}, use_global_device_ids=true | all-gather | bytes 393216 | tf_op jit(solution)/shard_map/all_gather | solution.py:44
  13.6 0.0 all-gather.2.cloned.1.call-update
  13.6 0.0 reduce-scatter.2.cloned.1.call-start
  14.4 0.7 fusion.17
  15.0 51.6 %all-gather.2.cloned.1.call-done = bf16[8192,256]{1,0:T(8,128)(2,1)} async-done(((bf16[512,256]{1,0:T(8,128)(2,1)}), bf16[8192,256]{1,0:T(8,128)(2,1)}) %all-gather.2.cloned.1.call-update) | async-done | bytes 4194320 | tf_op jit(solution)/shard_map/all_gather | solution.py:45
  66.6 2.8 gather_fusion
  69.4 0.0 copy-done
  69.4 0.3 fusion.10
  69.7 5.4 %all_gather.11 = bf16[512,256]{0,1:T(8,128)(2,1)S(1)} all-gather(bf16[256,256]{0,1:T(8,128)(2,1)S(1)} %fusion.10), channel_id=1, replica_groups=mesh['scen'=8,'rootr'=2,'rootc'=2] {'rootc'}, dimensions={0}, use_global_device_ids=true | all-gather | bytes 393216 | tf_op jit(solution)/shard_map/all_gather | solution.py:51
  75.2 0.0 copy-start.1
  75.2 0.0 copy-start.2
  75.2 0.0 copy-start.3
  75.2 2.5 convolution_bitcast_fusion
  77.7 0.0 reduce-scatter.2.cloned.1.call-update
  77.7 0.0 all-reduce.3.cloned.1.call-start
  77.7 16.4 %reduce-scatter.2.cloned.1.call-done = f32[768,128]{0,1:T(8,128)} async-done(((f32[768,256]{0,1:T(8,128)}), f32[768,128]{0,1:T(8,128)}) %reduce-scatter.2.cloned.1.call-update) | async-done | bytes 393232 | tf_op jit(solution)/shard_map/reduce_scatter | solution.py:54
  94.2 1.1 copy.11
  95.3 2.5 broadcast_in_dim.24
  97.8 2.6 scatter_fusion
  100.4 0.0 copy-done.1
  100.4 0.0 copy-done.2
  100.4 0.0 copy-done.3
  100.4 1.8 add_dynamic-update-slice_fusion
  102.2 0.0 all-reduce.3.cloned.1.call-update
  102.2 0.1 copy.12
  102.4 28.7 %all-reduce.3.cloned.1.call-done = f32[8192,128]{1,0:T(8,128)} async-done(((f32[8192,128]{1,0:T(8,128)}), f32[8192,128]{1,0:T(8,128)}) %all-reduce.3.cloned.1.call-update) | async-done | bytes 4194320 | tf_op jit(solution)/shard_map/psum | solution.py:65
  131.0 167.0 %all-reduce.4 = bf16[8192,128]{1,0:T(8,128)(2,1)S(1)} all-reduce(f32[8192,128]{1,0:T(8,128)} %all-reduce.3.cloned.1.call-done), channel_id=1, replica_groups=mesh['scen'=8,'rootr'=2,'rootc'=2] {'scen'}, use_global_device_ids=true, to_apply=%region_3.4 | all-reduce | flops 1048576 | bytes 6291456 | tf_op jit(solution)/shard_map/psum | solution.py:65
  298.1 6.3 %fusion.5 = f32[512,128]{0,1:T(8,128)S(1)} fusion(f32[512,128]{0,1:T(8,128)S(1)} %copy.12, bf16[512,8192]{1,0:T(8,128)(2,1)} %param.11, bf16[8192,128]{1,0:T(8,128)(2,1)S(1)} %all-reduce.4), kind=kOutput, calls=%fused_computation.8 | convolution fusion | flops 1073807360 | bytes 11010048 | tf_op jit(solution)/shard_map/dot_general | solution.py:67
  304.3 0.8 copy.13
  (2 shorter events, 0.0 us)
Async XLA Ops:
  6.5 62.9 %copy-start = (bf16[1,256,768]{2,1,0:T(8,128)(2,1)S(1)}, bf16[1,256,768]{2,1,0:T(8,128)(2,1)}, u32[]{:S(2)}) copy-start(bf16[1,256,768]{2,1,0:T(8,128)(2,1)} %param.12) | copy-start | bytes 1179652
  6.5 60.1 %all-gather.2.cloned.1.call-start = ((), (), s32[]{:S(2)}) async-start(), calls=%async_computation.1 | async-start | bytes 4456448 | tf_op jit(solution)/shard_map/all_gather | solution.py:45
  13.6 80.5 %reduce-scatter.2.cloned.1.call-start = ((), (), s32[]{:S(2)}) async-start(), calls=%async_computation.2 | async-start | bytes 1179648 | tf_op jit(solution)/shard_map/reduce_scatter | solution.py:54
  75.2 25.2 %copy-start.1 = (f32[512,128]{1,0:T(8,128)S(1)}, f32[512,128]{1,0:T(8,128)}, u32[]{:S(2)}) copy-start(f32[512,128]{1,0:T(8,128)} %param.8) | copy-start | bytes 786436
  75.2 25.2 %copy-start.2 = (f32[512,128]{1,0:T(8,128)S(1)}, f32[512,128]{1,0:T(8,128)}, u32[]{:S(2)}) copy-start(f32[512,128]{1,0:T(8,128)} %param.9) | copy-start | bytes 786436
  75.2 25.2 %copy-start.3 = (f32[512]{0:T(512)S(1)}, f32[512]{0:T(512)}, u32[]{:S(2)}) copy-start(f32[512]{0:T(512)} %param.10) | copy-start | bytes 6148
  77.7 53.4 %all-reduce.3.cloned.1.call-start = ((), (), s32[]{:S(2)}) async-start(), calls=%async_computation.3 | async-start | bytes 8388608 | tf_op jit(solution)/shard_map/psum | solution.py:65
Sparse Core Ops, SparseCore 0:
  13.8 52.8 all-gather.1
  77.8 16.3 reduce-scatter.1
  102.3 28.6 all-reduce.2
